TPU v7x, 32 devices: a 4x4x1 block of a 4x4x8 slice. The times are simulated.
32 devices in a mesh: rep: 1 (over z), dp: 32 (over x, y, core).
Axes of the slice: x: 4, y: 4, z: 1, core: 2. Of those that a mesh axis runs over, the one named last changes fastest.
The devices are a block of a 4x4x8 slice.
Arguments:
- g_w_gate: bfloat16 [32, 2, 896, 4864], P(('rep', 'dp'))
- g_w_up: bfloat16 [32, 2, 896, 4864], P(('rep', 'dp'))
- g_w_down: bfloat16 [32, 2, 4864, 896], P(('rep', 'dp'))
- w_gate: bfloat16 [2, 896, 4864], replicated
- w_up: bfloat16 [2, 896, 4864], replicated
- w_down: bfloat16 [2, 4864, 896], replicated
- m_w_gate: float32 [2, 896, 4864], P(None, 'dp')
- m_w_up: float32 [2, 896, 4864], P(None, 'dp')
- m_w_down: float32 [2, 4864, 896], P(None, 'dp')
- v_w_gate: float32 [2, 896, 4864], P(None, 'dp')
- v_w_up: float32 [2, 896, 4864], P(None, 'dp')
- v_w_down: float32 [2, 4864, 896], P(None, 'dp')
Outputs:
- output 1: bfloat16 [2, 896, 4864], P('rep')
- output 2: bfloat16 [2, 896, 4864], P('rep')
- output 3: bfloat16 [2, 4864, 896], P('rep')
- output 4: float32 [2, 896, 4864], P('rep', 'dp')
- output 5: float32 [2, 896, 4864], P('rep', 'dp')
- output 6: float32 [2, 4864, 896], P('rep', 'dp')
- output 7: float32 [2, 896, 4864], P('rep', 'dp')
- output 8: float32 [2, 896, 4864], P('rep', 'dp')
- output 9: float32 [2, 4864, 896], P('rep', 'dp')
All inputs are finite; a program needn't handle non-finite values.
Results may differ from a plain program's by a relative error of at most 0.022.
Values are sent between devices in bfloat16 or wider.
A program may use at most 768 MiB of HBM per device.

v0:
```python
import jax
import jax.numpy as jnp
from jax import lax
from jax.sharding import PartitionSpec as P


def adamw(w, m, v, g):
    m = 0.9 * m + 0.1 * g
    v = 0.95 * v + 0.05 * g * g
    step = m * lax.rsqrt(v + 1e-8) + 0.1 * w
    return (w - 0.02 * step).astype(jnp.bfloat16), m, v


def solution(mesh):
    def step(*arrays):
        terms, weights, m, v = (arrays[i : i + 3] for i in (0, 3, 6, 9))
        gradients = [lax.psum_scatter(t[0], "dp", scatter_dimension=1, tiled=True).astype(jnp.float32) for t in terms]
        me = lax.axis_index("dp")
        own = [lax.dynamic_slice_in_dim(w, me * one.shape[1], one.shape[1], 1).astype(jnp.float32) for w, one in zip(weights, m, strict=True)]
        new = [adamw(w, m, v, g) for w, m, v, g in zip(own, m, v, gradients, strict=True)]
        whole = [lax.all_gather(one[0], "dp", axis=1, tiled=True) for one in new]
        return (*whole, *(one[1] for one in new), *(one[2] for one in new))

    all_of, cut = P(None, None, None), P(None, "dp", None)
    return jax.shard_map(
        step,
        mesh=mesh,
        in_specs=(P(("rep", "dp"), None, None, None),) * 3 + (all_of,) * 3 + (cut,) * 6,
        out_specs=(P("rep", None, None),) * 3 + (P("rep", "dp", None),) * 6,
        check_vma=False,
    )
```

profile of v0, /device:TPU:97, one launch (start us, length us, event | category | flops | bytes accessed | tf_op | source)
XLA Modules:
  0.0 769.5 jit_solution(16171258063455724371)
XLA Ops:
  7.2 0.1 all-reduce.5.cloned.1.call-start
  7.3 67.2 %copy.47 = bf16[1,2,896,4864]{3,1,2,0:T(2,128)(2,1)} copy(bf16[1,2,896,4864]{3,2,1,0:T(8,128)(2,1)} %param.12) | data formatting | bytes 34865152 | tf_op args[0]
  74.5 0.1 all-reduce.5.cloned.1.call-update
  74.6 0.1 all-reduce.7.cloned.1.call-start
  74.6 67.3 %copy.46 = bf16[1,2,896,4864]{3,1,2,0:T(2,128)(2,1)} copy(bf16[1,2,896,4864]{3,2,1,0:T(8,128)(2,1)} %param.13) | data formatting | bytes 34865152 | tf_op args[1]
  141.9 0.1 all-reduce.7.cloned.1.call-update
  142.0 0.1 reduce-scatter.4.cloned.1.call-start
  142.0 77.0 %copy.33 = bf16[2,4864,896]{2,0,1:T(2,128)(2,1)S(1)} copy(bf16[2,4864,896]{2,1,0:T(8,128)(2,1)} %bitcast.15) | data formatting | bytes 34865152
  219.1 7.9 %copy.37 = bf16[608,8,2,896]{3,1,2,0:T(8,128)(2,1)} copy(bf16[608,8,2,896]{3,2,1,0:T(2,128)(2,1)S(1)} %bitcast.14) | data formatting | bytes 34865152
  227.0 0.0 copy-start.1
  227.0 0.1 reduce-scatter.4.cloned.1.call-update
  227.0 0.0 copy-start
  227.0 0.1 all-gather.4.cloned.1.call-start
  227.1 1.4 constant_dynamic-slice_fusion.1
  228.5 17.8 %all-reduce.5.cloned.1.call-done = bf16[2,896,4864]{2,0,1:T(2,128)(2,1)} async-done(((bf16[2,896,4864]{2,0,1:T(2,128)(2,1)}), bf16[2,896,4864]{2,0,1:T(2,128)(2,1)}) %all-reduce.5.cloned.1.call-update) | async-done | bytes 17432592
  246.3 0.0 copy-done.1
  246.3 0.0 copy-done
  246.3 5.6 fusion.13
  251.9 0.0 copy-start.2
  251.9 0.1 all-gather.4.cloned.1.call-update
  252.0 0.2 all-gather.6.cloned.1.call-start
  252.2 1.3 constant_dynamic-slice_fusion
  253.5 165.6 %all-reduce.7.cloned.1.call-done = bf16[2,896,4864]{2,0,1:T(2,128)(2,1)} async-done(((bf16[2,896,4864]{2,0,1:T(2,128)(2,1)}), bf16[2,896,4864]{2,0,1:T(2,128)(2,1)}) %all-reduce.7.cloned.1.call-update) | async-done | bytes 17432592
  419.1 0.0 copy-done.2
  419.1 0.0 copy-start.4
  419.1 5.7 fusion.14
  424.8 0.0 copy-start.3
  424.8 0.1 all-gather.6.cloned.1.call-update
  424.9 0.1 all-gather.8.cloned.1.call-start
  425.0 109.8 %reduce-scatter.4.cloned.1.call-done = bf16[152,1792]{1,0:T(8,128)(2,1)} async-done(((bf16[4864,1792]{1,0:T(8,128)(2,1)}), bf16[152,1792]{1,0:T(8,128)(2,1)}) %reduce-scatter.4.cloned.1.call-update) | async-done | bytes 544784
  534.8 1.2 reshape.19
  535.9 0.0 copy-done.4
  535.9 0.0 copy-done.3
  535.9 2.9 fusion.8
  538.8 0.1 all-gather.8.cloned.1.call-update
  538.9 68.5 %all-gather.4.cloned.1.call-done = bf16[2,896,4864]{2,0,1:T(2,128)(2,1)} async-done(((bf16[2,28,4864]{2,0,1:T(2,128)(2,1)}), bf16[2,896,4864]{2,0,1:T(2,128)(2,1)}) %all-gather.4.cloned.1.call-update) | async-done | bytes 17432592 | tf_op jit(solution)/shard_map/all_gather | solution.py:21
  607.4 15.6 %copy.31 = bf16[2,896,4864]{2,1,0:T(8,128)(2,1)} copy(bf16[2,896,4864]{2,0,1:T(2,128)(2,1)} %all-gather.4.cloned.1.call-done) | data formatting | bytes 34865152
  623.0 55.1 %all-gather.6.cloned.1.call-done = bf16[2,896,4864]{2,0,1:T(2,128)(2,1)} async-done(((bf16[2,28,4864]{2,0,1:T(2,128)(2,1)}), bf16[2,896,4864]{2,0,1:T(2,128)(2,1)}) %all-gather.6.cloned.1.call-update) | async-done | bytes 17432592 | tf_op jit(solution)/shard_map/all_gather | solution.py:21
  678.2 15.6 %copy.32 = bf16[2,896,4864]{2,1,0:T(8,128)(2,1)} copy(bf16[2,896,4864]{2,0,1:T(2,128)(2,1)} %all-gather.6.cloned.1.call-done) | data formatting | bytes 34865152
  693.8 54.6 %all-gather.8.cloned.1.call-done = bf16[2,4864,896]{2,1,0:T(8,128)(2,1)} async-done(((bf16[2,152,896]{2,1,0:T(8,128)(2,1)}), bf16[2,4864,896]{2,1,0:T(8,128)(2,1)}) %all-gather.8.cloned.1.call-update) | async-done | bytes 17432592 | tf_op jit(solution)/shard_map/all_gather | solution.py:21
  748.4 14.3 %copy.51 = bf16[2,4864,896]{2,1,0:T(8,128)(2,1)} copy(bf16[2,4864,896]{2,1,0:T(8,128)(2,1)} %all-gather.8.cloned.1.call-done) | data formatting | bytes 34865152
Async XLA Ops:
  7.2 239.1 %all-reduce.5.cloned.1.call-start = ((), (), s32[]{:S(2)}) async-start(), calls=%async_computation.5 | async-start | bytes 34865152
  74.6 344.5 %all-reduce.7.cloned.1.call-start = ((), (), s32[]{:S(2)}) async-start(), calls=%async_computation.6 | async-start | bytes 34865152
  142.0 392.8 %reduce-scatter.4.cloned.1.call-start = ((), (), s32[]{:S(2)}) async-start(), calls=%async_computation.4 | async-start | bytes 17977344
  227.0 19.4 %copy-start.1 = (f32[2,28,4864]{2,0,1:T(2,128)S(1)}, f32[2,28,4864]{2,0,1:T(2,128)}, u32[]{:S(2)}) copy-start(f32[2,28,4864]{2,0,1:T(2,128)} %param.18) | copy-start | bytes 3268612
  227.0 19.3 %copy-start = (f32[2,28,4864]{2,0,1:T(2,128)S(1)}, f32[2,28,4864]{2,0,1:T(2,128)}, u32[]{:S(2)}) copy-start(f32[2,28,4864]{2,0,1:T(2,128)} %param.21) | copy-start | bytes 3268612
  227.0 380.4 %all-gather.4.cloned.1.call-start = ((), (), s32[]{:S(2)}) async-start(), calls=%async_computation.1 | async-start | bytes 17977344 | tf_op jit(solution)/shard_map/all_gather | solution.py:21
  251.9 167.2 %copy-start.2 = (f32[2,28,4864]{2,0,1:T(2,128)S(1)}, f32[2,28,4864]{2,0,1:T(2,128)}, u32[]{:S(2)}) copy-start(f32[2,28,4864]{2,0,1:T(2,128)} %param.22) | copy-start | bytes 3268612
  252.0 426.2 %all-gather.6.cloned.1.call-start = ((), (), s32[]{:S(2)}) async-start(), calls=%async_computation.2 | async-start | bytes 17977344 | tf_op jit(solution)/shard_map/all_gather | solution.py:21
  419.1 116.8 %copy-start.4 = (f32[2,152,896]{2,1,0:T(8,128)S(1)}, f32[2,152,896]{2,1,0:T(8,128)}, u32[]{:S(2)}) copy-start(f32[2,152,896]{2,1,0:T(8,128)} %param.20) | copy-start | bytes 3268612
  424.8 111.1 %copy-start.3 = (f32[2,152,896]{2,1,0:T(8,128)S(1)}, f32[2,152,896]{2,1,0:T(8,128)}, u32[]{:S(2)}) copy-start(f32[2,152,896]{2,1,0:T(8,128)} %param.23) | copy-start | bytes 3268612
  424.9 323.5 %all-gather.8.cloned.1.call-start = ((), (), s32[]{:S(2)}) async-start(), calls=%async_computation.3 | async-start | bytes 17977344 | tf_op jit(solution)/shard_map/all_gather | solution.py:21
Sparse Core Ops, SparseCore 0:
  74.7 171.6 all-reduce.4
  250.7 168.3 all-reduce.6
  423.5 111.1 reduce-scatter.3
  537.3 70.0 all-gather.3
  610.0 68.1 all-gather.5
  680.2 68.1 all-gather.7
where the time goes:
time: 770 us; the launch traced here: 769 us
  waiting for transfers between devices  472 us (61%)
  local copies, waits for them, and re-layouts  269 us (35%)
  other arithmetic  14.2 us (2%)
  between operations  14.2 us (2%)
    unnamed x9, waiting for transfers between devices  293 us
    unnamed x18, local copies, waits for them, and re-layouts  266 us
    all_gather x3, waiting for transfers between devices, step(): whole = [lax.all_gather(one[0], 'dp', axis=1, tiled=True) for one in new]  178 us
  transfers between devices with their start and end apart: 6, of which 6 were waited for; matrix products, arithmetic and copies ran while one was open for 26% of the time, Pallas kernels for 0%

commit v1 on v0

v1 whole, which is shorter than its diff:
```python
import functools
import math

import jax
import jax.numpy as jnp
from jax import lax
from jax.experimental import pallas as pl
from jax.experimental.pallas import tpu as pltpu
from jax.sharding import PartitionSpec as P

MESH = pl.DeviceIdType.MESH
F32, BF16 = jnp.float32, jnp.bfloat16
STEP = 176
LANES, TILE = 128, 8
VMEM_MAIN = 14 * 2**20
WEIGHTS, CORES, KINDS = range(3), range(2), range(5)
DIRS = (1, -1)


def ranges(n):
    half = n // 4 // 16 * 16
    cuts = ((0, half), (half, half), (2 * half, half), (3 * half, n - 3 * half))
    return (cuts[:2], cuts[2:])


def loop(rows, body):
    full = rows // STEP
    if full == 1:
        body(0, STEP)
    elif full:
        lax.fori_loop(0, full, lambda i, _: (body(pl.multiple_of(i * STEP, 16), STEP), 0)[1], 0)
    if rows % STEP:
        body(full * STEP, rows % STEP)


def add_into(out, rows, terms, dtype=None):
    def body(at, size):
        here = pl.ds(at, size)
        total = terms[0][here, :].astype(F32)
        for term in terms[1:]:
            total += term[here, :].astype(F32)
        total = total.astype(BF16)
        out[here, :] = total if dtype is None else total.astype(dtype)

    loop(rows, body)


def moments(w, m, v, g):
    m = 0.9 * m + 0.1 * g
    v = 0.95 * v + 0.05 * g * g
    step = m * lax.rsqrt(v + 1e-8) + 0.1 * w
    return w - 0.02 * step, m, v


def kernel(side, block, forms, *refs):
    g, w, m, v, out, m_out, v_out = (refs[i : i + 3] for i in range(0, 21, 3))
    (own1, own2, grad, grad_p, w_raw, w_all, shared, mom,
     s_pair, r_pair, s_own1, s_own2, s_rs, r_p, r_q, s_in, s_grad, r_grad, s_x, r_x, s_out, s_ag, r_ag, s_fan, r_fan, free) = refs[21:]
    me = lax.axis_index("dp")
    c, y, x = me % 2, me // 2 % side, me // (2 * side)
    other = 1 - c
    pos = (x, y)
    cuts = ranges(block)
    span = [(cuts[i][0][0], cuts[i][0][1] + cuts[i][1][1]) for i in CORES]

    def at(p):
        return lax.rem(p + 2 * side, side)

    def device(axis, d):
        p = [x, y]
        p[axis] = at(pos[axis] + d)
        return {"dp": (p[0] * side + p[1]) * 2 + c}

    partner = {"dp": me + 1 - 2 * c}

    def land(k, core=None):
        return out[k].at[c if core is None else core]

    def t1(k, i, di):
        return out[k].at[other, 2, pl.ds(2 * di, 2), pl.ds(*span[i])]

    def r1(k, i, di, p):
        return out[k].at[other, di, p, pl.ds(*span[i])]

    def t2(k, i, d):
        return out[k].at[other, 3, 2, pl.ds(*cuts[i][int(d == 1)])]

    def r2(k, i, di, h):
        return out[k].at[other, 3, di, pl.ds(*cuts[i][h])]

    def remote(src, dst, send, recv, to):
        return pltpu.make_async_remote_copy(src, dst, send, recv, device_id=to, device_id_type=MESH)

    def local(src, dst, sem):
        return pltpu.make_async_copy(src, dst, sem)

    def most(k):
        return w[k].at[0, pl.ds(0, side * side - 1)]

    neighbours = [device(i, d) for i in CORES for d in DIRS]
    barrier = pltpu.get_barrier_semaphore()
    for to in (partner, *neighbours):
        pl.semaphore_signal(barrier, inc=1, device_id=to, device_id_type=MESH)
    pl.semaphore_wait(barrier, 1 + len(neighbours))

    def pair_of_blocks(ref, i, p, h):
        lo, n = span[i]
        rows = pl.ds(lo, n)
        return ref.at[p, pl.ds(2 * h, 2), rows] if i == 0 else ref.at[pl.ds(2 * h, 2), p, rows]

    def row_of_blocks(ref, i):
        lo, n = span[i]
        rows = pl.ds(lo, n)
        return ref.at[pos[0], :, rows] if i == 0 else ref.at[:, pos[1], rows]

    pieces = [(i, d) for d in DIRS for i in CORES]

    def target(s, i, d):
        hf = 1 if d == 1 else 0
        return (at(pos[i] + 2), hf) if s == 0 else (at(pos[i] + d), 1 - hf if s == 1 else hf)

    def pair_copy(k, j):
        if j < 12:
            i, d = pieces[j % 4]
            p, h = target(j // 4, i, d)
            view = functools.partial(pair_of_blocks, i=i, p=p, h=h)
        else:
            view = functools.partial(row_of_blocks, i=j - 12)
        return remote(view(g[k].at[other]), view(land(k, other)), s_pair.at[k], r_pair.at[k, j], partner)

    order1 = [(k, s, i, d) for k in WEIGHTS for s in range(3) for i, d in pieces]

    def own1_copy(n):
        k, s, i, d = order1[n]
        p, h = target(s, i, d)
        return local(pair_of_blocks(g[k].at[c], i, p, h), own1.at[n % 4, :, pl.ds(0, span[i][1])], s_own1.at[n % 4])

    def own2_copy(k, i):
        return local(row_of_blocks(g[k].at[c], i), own2.at[i, :, pl.ds(0, span[i][1])], s_own2.at[i])

    def p_copy(k, s, i, d):
        di = DIRS.index(d)
        p, h = target(s, i, d)
        dst = t1(k, i, di) if s == 0 else r1(k, i, di, pl.ds(2 * h, 2))
        return remote(pair_of_blocks(land(k), i, p, h), dst, s_rs.at[k], r_p.at[k, s, i, di], device(i, d))

    def stage_p(k, s):
        for j, (i, d) in enumerate(pieces):
            n = order1.index((k, s, i, d))
            if n + 3 < len(order1):
                own1_copy(n + 3).start()
            own1_copy(n).wait()
            pair_copy(k, s * 4 + j).wait_recv()
            if s == 2:
                p_copy(k, 0, i, d).wait_recv()
            p, h = target(s, i, d)
            sums = pair_of_blocks(land(k), i, p, h)
            for b in CORES:
                terms = [own1.at[n % 4, b], sums.at[b]]
                if s == 2:
                    terms.append(t1(k, i, DIRS.index(d)).at[b])
                add_into(sums.at[b], span[i][1], terms)
            p_copy(k, s, i, d).start()

    def q_target(s, i, d):
        hf = 1 if d == 1 else 0
        p = pos[1 - i]
        return (at(p + 2), hf) if s == 0 else (at(p + d), 1 - hf if s == 1 else hf)

    def q_rows(ref, i, p, h):
        lo, n = cuts[i][h]
        return (ref.at[pos[0], p] if i == 0 else ref.at[p, pos[1]]).at[pl.ds(lo, n)]

    def q_copy(k, s, i, d):
        di = DIRS.index(d)
        p, h = q_target(s, i, d)
        dst = t2(k, i, d) if s == 0 else r2(k, i, di, h)
        return remote(q_rows(land(k), i, p, h), dst, s_rs.at[k], r_q.at[k, s, i, di], device(1 - i, d))

    def q_terms(k, i, p, h):
        off, n = cuts[i][h][0] - span[i][0], cuts[i][h][1]
        rows = pl.ds(off, n)
        return [own2.at[i, p, rows], q_rows(land(k), i, p, h)] + [r1(k, i, di, p).at[rows] for di in CORES]

    def stage_q(k, s):
        if s == 0:
            for i in CORES:
                own2_copy(k, i).wait()
                pair_copy(k, 12 + i).wait_recv()
            for i, d in pieces:
                p_copy(k, 1, i, d).wait_recv()
                p_copy(k, 2, i, d).wait_recv()
        for i, d in pieces:
            p, h = q_target(s, i, d)
            terms = q_terms(k, i, p, h)
            if s == 2:
                q_copy(k, 0, i, d).wait_recv()
                terms.append(t2(k, i, d))
            add_into(q_rows(land(k), i, p, h), cuts[i][h][1], terms)
            q_copy(k, s, i, d).start()

    def step_loads(k):
        return [local(w[k].at[:, x * side + y], w_raw, s_in.at[0]), local(m[k], mom.at[0], s_in.at[1]), local(v[k], mom.at[1], s_in.at[2])]

    def step_stores(k):
        return [local(mom.at[0], m_out[k], s_out.at[0]), local(mom.at[1], v_out[k], s_out.at[1])]

    def own_rows(k, core):
        rows, lanes = forms[k]
        if rows % TILE == 0:
            return core * (rows * lanes), rows * lanes
        return core * (rows // TILE * TILE * lanes), (rows // TILE + 1) * TILE * lanes

    def grad_copy(k):
        lo, n = own_rows(k, other)
        rows = pl.ds(pl.multiple_of(lo, 8), n)
        return remote(grad.at[rows], grad_p.at[rows], s_grad.at[k], r_grad.at[k], partner)

    def x_copies(k):
        rows, lanes = forms[k]
        lo, n = own_rows(k, c)
        if rows % TILE == 0:
            mine = pl.ds(pl.multiple_of(lo, 8), n)
            return [remote(w_all.at[other, mine], w_all.at[other, mine], s_x.at[k, 0], r_x.at[k, 0], partner)]
        tile = TILE * lanes
        mine = pl.ds(pl.multiple_of(c * (n - 2 * tile + 2 * tile), 8), n - tile)
        middle = pl.ds(n - tile, tile)
        return [
            remote(w_all.at[other, mine], w_all.at[other, mine], s_x.at[k, 0], r_x.at[k, 0], partner),
            remote(w_all.at[other, middle], shared, s_x.at[k, 1], r_x.at[k, 1], partner),
        ]

    def take_step(k):
        rows, lanes = forms[k]

        def update(core):
            grads = (grad, grad_p) if core == 0 else (grad_p, grad)

            def one(layer, at_w, at_m):
                new_w, new_m, new_v = moments(w_all[layer, at_w, :], mom[0, at_m, :], mom[1, at_m, :], grads[layer][at_w, :])
                w_all[layer, at_w, :] = new_w
                mom[0, at_m, :] = new_m
                mom[1, at_m, :] = new_v

            if rows % TILE == 0:
                size = rows * lanes
                chunk = 8 * (rows // TILE)

                def body(n, _):
                    for layer in CORES:
                        one(layer, pl.ds(pl.multiple_of(core * size + n * chunk, 8), chunk), pl.ds(pl.multiple_of(layer * size + n * chunk, 8), chunk))
                    return 0

                lax.fori_loop(0, lanes, body, 0)
            else:
                first, last = core * rows, (core + 1) * rows
                parts = []
                r = first
                while r < last:
                    n = min(8 - r % 8, last - r)
                    parts.append((r, n))
                    r += n

                def body(lane, _):
                    for layer in CORES:
                        for r, n in parts:
                            one(layer, pl.ds((r // TILE * lanes + lane) * 8 + r % 8, n), pl.ds((r - first) * 2 * lanes + lane * 2 + layer, n, stride=2 * lanes))
                    return 0

                lax.fori_loop(0, lanes, body, 0)

        for core in CORES:
            pl.when(c == core)(functools.partial(update, core))

    def stage_step(k):
        loads = step_loads(k)
        loads[0].wait()
        for layer in CORES:

            def widen(start, size, layer=layer):
                w_all[layer, pl.ds(start, size), :] = w_raw[layer, pl.ds(start, size), :].astype(F32)

            loop(block, widen)
        for i, d in pieces:
            q_copy(k, 1, i, d).wait_recv()
            q_copy(k, 2, i, d).wait_recv()
        for i in CORES:
            for h in CORES:
                lo, n = cuts[i][h]
                terms = q_terms(k, i, pos[1 - i], h) + [r2(k, i, di, h) for di in CORES]
                add_into(grad.at[pl.ds(lo, n)], n, terms, F32)
        grad_copy(k).start()
        local(most(k), most(k), s_rs.at[k]).wait()
        for to in neighbours:
            pl.semaphore_signal(free.at[k], inc=1, device_id=to, device_id_type=MESH)
        loads[1].wait()
        loads[2].wait()
        grad_copy(k).wait_recv()
        take_step(k)
        for copy in step_stores(k):
            copy.start()
        swaps = x_copies(k)
        for copy in swaps:
            copy.start()
        for copy in swaps:
            copy.wait()
        rows, lanes = forms[k]
        if rows % TILE:
            tile = TILE * lanes
            start = rows // TILE * tile

            def merge(n, _):
                here = pl.ds(pl.multiple_of(start + n * 8, 8), 8)
                theirs = shared[pl.ds(pl.multiple_of(n * 8, 8), 8), :]
                mine = w_all[c, here, :]
                low = lax.broadcasted_iota(jnp.int32, theirs.shape, 0) < rows % TILE
                w_all[c, here, :] = jnp.where(low == (c == 0), mine, theirs)
                return 0

            lax.fori_loop(0, lanes, merge, 0)

        def narrow(start, size):
            out[k][c, x, y, pl.ds(start, size), :] = w_all[c, pl.ds(start, size), :].astype(BF16)

        loop(block, narrow)
        grad_copy(k).wait_send()
        for copy in step_stores(k):
            copy.wait()

    def place(i, first, second):
        return (second, first) if i == 0 else (first, second)

    def rows_of(i, h):
        return pl.ds(*(span[i] if h is None else cuts[i][h]))

    def ag_copy(k, i, along, d, first, second, h, event):
        dst = out[k].at[c, *place(i, first, second), rows_of(i, h)]
        return remote(dst, dst, s_ag.at[k], r_ag.at[k, i, event], device(1 - i if along == 0 else i, d))

    def fan(k, i, first, second, h):
        there = out[k].at[c, *place(i, first, second), rows_of(i, h)]
        remote(there, there, s_fan.at[k], r_fan.at[k], partner).start()

    def arrived(k, i, first, second, h, event):
        ag_copy(k, i, 0, 1, first, second, h, event).wait_recv()

    def ag_own(k):
        src = out[k].at[c, x, y]
        pl.semaphore_wait(free.at[k], len(neighbours))
        for i in CORES:
            f, s = pos[1 - i], pos[i]
            for di, d in enumerate(DIRS):
                ag_copy(k, i, 0, d, f, s, None, di).start()
            for di, d in enumerate(DIRS):
                ag_copy(k, i, 1, d, f, s, None, 4 + 5 * di).start()
        remote(src, src, s_fan.at[k], r_fan.at[k], partner).start()

    def ag_near(k):
        for di, d in enumerate(DIRS):
            for i in CORES:
                f, s = pos[1 - i], pos[i]
                from_ = at(f - d)
                arrived(k, i, from_, s, None, di)
                ag_copy(k, i, 0, d, from_, s, 1 - di, 2 + di).start()
                for d2i, d2 in enumerate(DIRS):
                    ag_copy(k, i, 1, d2, from_, s, None, 4 + 5 * d2i + 1 + di).start()
                fan(k, i, from_, s, None)

    def ag_far(k):
        for di, d in enumerate(DIRS):
            for i in CORES:
                f, s = pos[1 - i], pos[i]
                arrived(k, i, at(f + 2), s, 1 - di, 2 + di)
                for d2i, d2 in enumerate(DIRS):
                    ag_copy(k, i, 1, d2, at(f + 2), s, 1 - di, 4 + 5 * d2i + 3 + 1 - di).start()
                fan(k, i, at(f + 2), s, 1 - di)

    kinds = ((0, None, 0, 14), (-1, None, 0, 15), (1, None, 1, 16), (2, 0, 1, 17), (2, 1, 1, 18))

    def ag_second(k, which):
        for n in which:
            rel, h, onward, event = kinds[n]
            for di, d in enumerate(DIRS):
                for i in CORES:
                    f, s = pos[1 - i], pos[i]
                    first, second = at(f + rel), at(s - d)
                    arrived(k, i, first, second, h, 4 + 5 * di + n)
                    if di == onward:
                        ag_copy(k, i, 1, d, first, second, h, event).start()
                    fan(k, i, first, second, h)

    def ag_last(k):
        for n in (0, 2, 1, 3, 4):
            rel, h, _, event = kinds[n]
            for i in CORES:
                f, s = pos[1 - i], pos[i]
                arrived(k, i, at(f + rel), at(s + 2), h, event)
                fan(k, i, at(f + rel), at(s + 2), h)

    for n in range(3):
        own1_copy(n).start()
    for k in WEIGHTS:
        for j in range(14):
            pair_copy(k, j).start()

    def q12(k):
        for copy in step_loads(k):
            copy.start()
        stage_q(k, 0)
        stage_q(k, 1)

    def q3(k):
        stage_q(k, 2)

    def step(k):
        stage_step(k)
        if k < 2:
            for i in CORES:
                own2_copy(k + 1, i).start()

    for i in CORES:
        own2_copy(0, i).start()
    stage_p(0, 0), stage_p(0, 1), stage_p(0, 2), stage_p(1, 0), stage_p(1, 1)
    q12(0), stage_p(1, 2), q3(0), stage_p(2, 0), stage_p(2, 1), step(0)
    ag_own(0), q12(1), stage_p(2, 2), q3(1), ag_near(0), step(1)
    ag_own(1), q12(2), ag_far(0), q3(2), ag_second(0, (0, 1, 2)), step(2)
    ag_own(2), ag_second(0, (3, 4)), ag_near(1), ag_far(1), ag_near(2), ag_last(0), ag_second(1, KINDS), ag_far(2), ag_last(1)
    ag_second(2, KINDS), ag_last(2)

    for k in WEIGHTS:
        whole = land(k)
        local(whole, whole, s_pair.at[k]).wait()
        local(most(k), most(k), s_ag.at[k]).wait()
        local(whole, whole, s_fan.at[k]).wait()
        local(whole, whole, r_fan.at[k]).wait()


def spread(*refs):
    n = (len(refs) - 3) // 2
    buffer, s_in, s_out = refs[2 * n :]
    lanes = buffer.shape[2]
    for a in range(n):

        def load(lane, _, a=a):
            columns = pl.ds(pl.multiple_of(lane * LANES, LANES), LANES)
            pltpu.make_async_copy(refs[a].at[:, :, columns], buffer.at[a, :, lane], s_in.at[a]).start()
            return 0

        lax.fori_loop(0, lanes, load, 0)
    for a in range(n):
        pltpu.make_async_copy(refs[n + a], buffer.at[a], s_in.at[a]).wait()
        pltpu.make_async_copy(buffer.at[a], refs[n + a], s_out.at[a]).start()
    for a in range(n):
        pltpu.make_async_copy(buffer.at[a], refs[n + a], s_out.at[a]).wait()


def deliver(*refs):
    n = (len(refs) - 4) // 2
    src, dst, (buffer, s_w, s_in, s_out) = refs[:n], refs[n : 2 * n], refs[2 * n :]
    big = len(WEIGHTS)

    def load(j):
        return pltpu.make_async_copy(src[big + j], buffer.at[j], s_in.at[j])

    def store(j):
        return pltpu.make_async_copy(buffer.at[j], dst[big + j], s_out.at[j])

    for j in range(n - big):
        load(j).start()
    for k in WEIGHTS:
        for core in CORES:
            for x in range(src[k].shape[1]):
                pltpu.make_async_copy(src[k].at[core, x], dst[k].at[core, x], s_w.at[k]).start()
    for j in range(n - big):
        load(j).wait()
        store(j).start()
    for j in range(n - big):
        store(j).wait()
    for k in WEIGHTS:
        pltpu.make_async_copy(src[k], dst[k], s_w.at[k]).wait()


def tiles(a, chips):
    layers, rows, columns = a.shape
    a = a.reshape(layers, rows // TILE, TILE, columns // LANES, LANES).transpose(0, 1, 3, 2, 4)
    return a.reshape(layers, chips, -1, LANES)


def untiles(a, shape):
    layers, rows, columns = shape
    a = a.reshape(layers, rows // TILE, columns // LANES, TILE, LANES).transpose(0, 1, 3, 2, 4)
    return a.reshape(shape)


def moment_rows(arrays):
    odd = [a.transpose(1, 0, 2) for a in arrays if a.shape[1] % TILE]
    shapes = [(a.shape[0], a.shape[2] // LANES, a.shape[1], LANES) for a in odd]
    dma = pltpu.SemaphoreType.DMA((len(odd),))
    done = iter(
        pl.pallas_call(
            spread,
            out_shape=[jax.ShapeDtypeStruct(shape, F32) for shape in shapes],
            in_specs=[pl.BlockSpec(memory_space=pl.ANY)] * len(odd),
            out_specs=[pl.BlockSpec(memory_space=pl.ANY)] * len(odd),
            scratch_shapes=[pltpu.VMEM((len(odd), *shapes[0]), F32), dma, dma],
        )(*odd)
    )
    return [next(done).reshape(-1, LANES) if a.shape[1] % TILE else tiles(a, 1).reshape(-1, LANES) for a in arrays]


def moment_back(a, shape):
    layers, rows, columns = shape
    if rows % TILE == 0:
        return untiles(a, shape)
    return a.reshape(rows, columns // LANES, layers, 128).transpose(0, 2, 1, 3).reshape(rows, layers, columns).transpose(1, 0, 2)


def solution(mesh):
    n = mesh.shape["dp"]
    side = math.isqrt(n // 2)
    chips = side * side
    assert 2 * chips == n and side == 4

    def step(*arrays):
        terms, weights, m, v = (arrays[i : i + 3] for i in (0, 3, 6, 9))
        shapes, m_shapes = [a.shape for a in weights], [a.shape for a in m]
        block = math.prod(shapes[0][1:]) // chips // LANES
        forms = [(s[1], s[2] // LANES) for s in m_shapes]
        cuts = ranges(block)
        wide = max(sum(h[1] for h in i) for i in cuts)
        odd = max([lanes * TILE for rows, lanes in forms if rows % TILE] + [8])
        split = (2, side, side, block, LANES)
        operands = (
            [tiles(t[0], chips).reshape(split) for t in terms] + [tiles(a, chips) for a in weights] + moment_rows(m + v)
        )
        dma = pltpu.SemaphoreType.DMA
        moment = jax.ShapeDtypeStruct(operands[6].shape, F32)
        anywhere = pl.BlockSpec(memory_space=pl.ANY)
        made = pl.pallas_call(
            functools.partial(kernel, side, block, forms),
            out_shape=[pltpu.VMEM(split, BF16)] * 3 + [moment] * 6,
            in_specs=[anywhere] * 12,
            out_specs=[pl.BlockSpec(memory_space=pltpu.VMEM)] * 3 + [anywhere] * 6,
            scratch_shapes=[
                pltpu.VMEM((4, 2, wide, LANES), BF16),
                pltpu.VMEM((2, side, wide, LANES), BF16),
                pltpu.VMEM((block, LANES), F32),
                pltpu.VMEM((block, LANES), F32),
                pltpu.VMEM((2, block, LANES), BF16),
                pltpu.VMEM((2, block, LANES), F32),
                pltpu.VMEM((odd, LANES), F32),
                pltpu.VMEM((2, *moment.shape), F32),
                *(dma(shape) for shape in ((3,), (3, 14), (4,), (2,), (3,), (3, 3, 2, 2), (3, 3, 2, 2), (3,), (3,), (3,), (3, 2), (3, 2), (2,), (3,), (3, 2, 19), (3,), (3,))),
                pltpu.SemaphoreType.REGULAR((3,)),
            ],
            compiler_params=pltpu.CompilerParams(collective_id=0, has_side_effects=True, vmem_limit_bytes=VMEM_MAIN),
        )(*operands)
        made = [*(pltpu.with_memory_space_constraint(a, pltpu.VMEM) for a in made[:3]), *made[3:]]
        results = pl.pallas_call(
            deliver,
            out_shape=[jax.ShapeDtypeStruct(a.shape, a.dtype) for a in made],
            in_specs=[anywhere] * 9,
            out_specs=[anywhere] * 9,
            scratch_shapes=[pltpu.VMEM((6, *moment.shape), F32), dma((3,)), dma((6,)), dma((6,))],
            compiler_params=pltpu.CompilerParams(vmem_limit_bytes=VMEM_MAIN),
        )(*made)
        new = [untiles(a, s) for a, s in zip(results[:3], shapes, strict=True)]
        return (*new, *(moment_back(a, s) for a, s in zip(results[3:], m_shapes * 2, strict=True)))

    all_of, cut = P(None, None, None), P(None, "dp", None)
    return jax.shard_map(
        step,
        mesh=mesh,
        in_specs=(P(("rep", "dp"), None, None, None),) * 3 + (all_of,) * 3 + (cut,) * 6,
        out_specs=(P("rep", None, None),) * 3 + (P("rep", "dp", None),) * 6,
        check_vma=False,
    )
```

time: 770 us -> 308 us (0.40)
  waiting for transfers between devices: 472 us -> 0 us
  Pallas kernels: 0 us -> 307 us
  local copies, waits for them, and re-layouts: 269 us -> 0 us
  other arithmetic: 14.2 us -> 0 us
  between operations: 14.2 us -> 0.66 us
    pallas_call x0 -> x3, Pallas kernels: none -> 307 us  [the longest x1 282 us: step(): pl.pallas_call(functools.partial(kernel, side, block, forms), out_shape=[...]
    unnamed x9 -> x0, waiting for transfers between devices: 293 us -> none
    unnamed x18 -> x0, local copies, waits for them, and re-layouts: 266 us -> none
    all_gather x3 -> x0, waiting for transfers between devices: 178 us -> none  [step(): whole = [lax.all_gather(one[0], 'dp', axis=1, tiled=True) for one in new]]
    convert_element_type x3 -> x0, other arithmetic: 14.2 us -> none  [adamw(): return ((w - 0.02 * step).astype(jnp.bfloat16), m, v)]
  transfers between devices with their start and end apart: 6 -> 0, of which waited for: 6 -> 0; matrix products, arithmetic and copies ran while one was open for 26% -> 0% of each run, Pallas kernels for 0% -> 0%
where the time goes in v1:
time: 308 us; the launch traced here: 307 us
  Pallas kernels  307 us (100%)
    pallas_call x1, Pallas kernels, step(): pl.pallas_call(functools.partial(kernel, side, block, forms), out_shape=[...  282 us
    pallas_call x1, Pallas kernels, step(): pl.pallas_call(deliver, out_shape=[jax.ShapeDtypeStruct(a.shape, a.dtype)...  20.4 us

profile of v1, /device:TPU:97, one launch (start us, length us, event | category | flops | bytes accessed | tf_op | source)
XLA Modules:
  0.0 307.4 jit_solution(9100265163789427166)
XLA Ops:
  0.6 4.6 %shard_map.187 = (f32[28,38,2,128]{3,2,1,0:T(2,128)}, f32[28,38,2,128]{3,2,1,0:T(2,128)}, f32[28,38,2,128]{3,2,1,0:T(2,128)}, f32[28,38,2,128]{3,2,1,0:T(2,128)}) custom-call(f32[28,2,4864]{2,1,0:T(2,128)} %bitcast.107, f32[28,2,4864]{2,1,0:T(2,128)} %bitcast.108, f32[28,2,4864]{2,1,0:T(2,128)} %bitcast.109, f32[28,2,4864]{2,1,0:T(2,128)} %bitcast.110), custom_call_target="tpu_custom_call" | custom-call | tf_op jit(solution)/shard_map/pallas_call | solution.py:500
  5.2 281.8 %shard_map.188 = (bf16[2,4,4,2128,128]{4,3,2,1,0:T(8,128)(2,1)S(1)}, bf16[2,4,4,2128,128]{4,3,2,1,0:T(8,128)(2,1)S(1)}, bf16[2,4,4,2128,128]{4,3,2,1,0:T(8,128)(...) custom-call(bf16[2,4,4,2128,128]{4,3,2,1,0:T(8,128)(2,1)} %bitcast.1, ...), custom_call_target="tpu_custom_call" | custom-call | tf_op jit(solution)/shard_map/pallas_call | solution.py:539
  287.0 20.4 %shard_map.189 = (bf16[2,4,4,2128,128]{4,3,2,1,0:T(8,128)(2,1)}, bf16[2,4,4,2128,128]{4,3,2,1,0:T(8,128)(2,1)}, bf16[2,4,4,2128,128]{4,3,2,1,0:T(8,128)(2,1)}, f...) custom-call(bf16[2,4,4,2128,128]{4,3,2,1,0:T(8,128)(2,1)S(1)} %get-t, ...), custom_call_target="tpu_custom_call" | custom-call | tf_op jit(solution)/shard_map/pallas_call | solution.py:559

commit v2 on v1

v2 whole, which is shorter than its diff:
```python
import functools
import math

import jax
import jax.numpy as jnp
from jax import lax
from jax.experimental import pallas as pl
from jax.experimental.layout import Layout, with_layout_constraint
from jax.experimental.pallas import tpu as pltpu
from jax.sharding import PartitionSpec as P

MESH = pl.DeviceIdType.MESH
F32, BF16 = jnp.float32, jnp.bfloat16
STEP, SLOTS = 176, 4
LANES, TILE = 128, 8
VMEM_MAIN = 10116 * 2**10
IN_HBM = 1
WEIGHTS, CORES = range(3), range(2)
DIRS = (1, -1)
SCHEDULE = (
    "P00 P01 P02 P10",
    "P11 Q00 Q01 P12",
    "Q02 P20 P21 F0",
    "Q10 Q11 O0 P22",
    "Q12 N0 F1 Q20",
    "S02 X0 Q21 Q22",
    "O1 N1 S01 F2",
    "S00 O2 S03 S04",
    "L02 X1 L01 S10",
    "N2 L04 L00 S14",
    "L03 S11 S12 S13",
    "X2 S20 L10 L14",
    "L13 L12 L11 S21",
    "S22 S23 S24 L21",
    "L20 L22 L23 L24",
)


def ranges(n, k):
    half = n // 4 // 16 * 16
    rows = [half] * 4
    rows[1 + 2 * ((k + 1) % 2)] += n - 4 * half
    cuts = [(sum(rows[:j]), rows[j]) for j in range(4)]
    return (cuts[:2], cuts[2:])


def loop(rows, body):
    full = rows // STEP
    if full == 1:
        body(0, STEP)
    elif full:
        lax.fori_loop(0, full, lambda i, _: (body(pl.multiple_of(i * STEP, 16), STEP), 0)[1], 0)
    if rows % STEP:
        body(full * STEP, rows % STEP)


def add_into(out, rows, terms, dtype=None):
    def body(at, size):
        here = pl.ds(at, size)
        total = terms[0][here, :].astype(F32)
        for term in terms[1:]:
            total += term[here, :].astype(F32)
        total = total.astype(BF16)
        out[here, :] = total if dtype is None else total.astype(dtype)

    loop(rows, body)


def moments(w, m, v, g):
    m = 0.9 * m + 0.1 * g
    v = 0.95 * v + 0.05 * g * g
    step = m * lax.rsqrt(v + 1e-8) + 0.1 * w
    return w - 0.02 * step, m, v


def kernel(side, block, forms, *refs):
    g, w, m, v, out, m_out, v_out = (refs[i : i + 3] for i in range(0, 21, 3))
    (own1, own2, grad, grad_p, w_raw, w_all, shared,
     s_pair, r_pair, s_own1, s_own2, s_rs, r_p, r_q, s_in, s_grad, r_grad, s_x, r_x, s_out, s_ag, r_ag, s_fan, r_fan, r_first, free) = refs[21:]
    me = lax.axis_index("dp")
    c, y, x = me % 2, me // 2 % side, me // (2 * side)
    other = 1 - c
    pos = (x, y)
    cuts = [ranges(block, k) for k in WEIGHTS]
    span = [[(i[0][0], i[0][1] + i[1][1]) for i in cuts[k]] for k in WEIGHTS]

    def at(p):
        return lax.rem(p + 2 * side, side)

    def device(axis, d):
        p = [x, y]
        p[axis] = at(pos[axis] + d)
        return {"dp": (p[0] * side + p[1]) * 2 + c}

    partner = {"dp": me + 1 - 2 * c}

    def land(k, core=None):
        return out[k].at[c if core is None else core]

    def t1(k, i, di):
        return out[k].at[other, 2, pl.ds(2 * di, 2), pl.ds(*span[k][i])]

    def r1(k, i, di, p):
        return out[k].at[other, di, p, pl.ds(*span[k][i])]

    def t2(k, i, d):
        return out[k].at[other, 3, 2, pl.ds(*cuts[k][i][int(d == 1)])]

    def r2(k, i, di, h):
        return out[k].at[other, 3, di, pl.ds(*cuts[k][i][h])]

    def remote(src, dst, send, recv, to):
        return pltpu.make_async_remote_copy(src, dst, send, recv, device_id=to, device_id_type=MESH)

    def local(src, dst, sem):
        return pltpu.make_async_copy(src, dst, sem)

    def most(k):
        return w[k].at[0, pl.ds(0, side * side - 1)]

    def pair_of_blocks(ref, k, i, p, h):
        lo, n = span[k][i]
        rows = pl.ds(lo, n)
        return ref.at[p, pl.ds(2 * h, 2), rows] if i == 0 else ref.at[pl.ds(2 * h, 2), p, rows]

    def row_of_blocks(ref, k, i):
        lo, n = span[k][i]
        rows = pl.ds(lo, n)
        return ref.at[pos[0], :, rows] if i == 0 else ref.at[:, pos[1], rows]

    pieces = [(i, d) for d in DIRS for i in CORES]

    def target(s, i, d):
        hf = 1 if d == 1 else 0
        return (at(pos[i] + 2), hf) if s == 0 else (at(pos[i] + d), 1 - hf if s == 1 else hf)

    def pair_copy(k, j):
        if j < 12:
            i, d = pieces[j % 4]
            p, h = target(j // 4, i, d)
            view = functools.partial(pair_of_blocks, k=k, i=i, p=p, h=h)
        else:
            view = functools.partial(row_of_blocks, k=k, i=j - 12)
        return remote(view(g[k].at[other]), view(land(k, other)), s_pair.at[k], r_pair.at[k, j], partner)

    quarters = [(b, h) for b in CORES for h in CORES]

    def quarter(ref, i, d, b, h):
        p, half = target(0, i, d)
        rows = pl.ds(*cuts[0][i][h])
        return ref.at[p, 2 * half + b, rows] if i == 0 else ref.at[2 * half + b, p, rows]

    def first_pair(i, d, b, h):
        return remote(quarter(g[0].at[other], i, d, b, h), quarter(land(0, other), i, d, b, h), s_pair.at[0], r_first.at[0, i, DIRS.index(d), b, h], partner)

    def first_send(i, d, b, h):
        lo, n = cuts[0][i][h]
        dst = t1(0, i, DIRS.index(d)).at[b, pl.ds(lo - span[0][i][0], n)]
        return remote(quarter(land(0), i, d, b, h), dst, s_rs.at[0], r_first.at[1, i, DIRS.index(d), b, h], device(i, d))

    def stage_first():
        for b, h in quarters:
            for j, (i, d) in enumerate(pieces):
                if (b, h) == quarters[0]:
                    own1_copy(j).wait()
                first_pair(i, d, b, h).wait_recv()
                lo, n = cuts[0][i][h]
                sums = quarter(land(0), i, d, b, h)
                add_into(sums, n, [own1.at[j % SLOTS, b, pl.ds(lo - span[0][i][0], n)], sums])
                first_send(i, d, b, h).start()
        for n in range(SLOTS, 2 * SLOTS - 1):
            own1_copy(n).start()

    order1 = [(k, s, i, d) for k in WEIGHTS for s in range(3) for i, d in pieces]

    def own1_copy(n):
        k, s, i, d = order1[n]
        p, h = target(s, i, d)
        return local(pair_of_blocks(g[k].at[c], k, i, p, h), own1.at[n % SLOTS, :, pl.ds(0, span[k][i][1])], s_own1.at[n % SLOTS])

    def own2_copy(k, i):
        return local(row_of_blocks(g[k].at[c], k, i), own2.at[i, :, pl.ds(0, span[k][i][1])], s_own2.at[i])

    def p_copy(k, s, i, d):
        di = DIRS.index(d)
        p, h = target(s, i, d)
        dst = t1(k, i, di) if s == 0 else r1(k, i, di, pl.ds(2 * h, 2))
        return remote(pair_of_blocks(land(k), k, i, p, h), dst, s_rs.at[k], r_p.at[k, s, i, di], device(i, d))

    def stage_p(k, s):
        if k + s == 0:
            return stage_first()
        for j, (i, d) in enumerate(pieces):
            n = order1.index((k, s, i, d))
            if n + SLOTS - 1 < len(order1):
                own1_copy(n + SLOTS - 1).start()
            own1_copy(n).wait()
            pair_copy(k, s * 4 + j).wait_recv()
            if s == 2 and k == 0:
                for b, h in quarters:
                    first_send(i, d, b, h).wait_recv()
            elif s == 2:
                p_copy(k, 0, i, d).wait_recv()
            p, h = target(s, i, d)
            sums = pair_of_blocks(land(k), k, i, p, h)
            for b in CORES:
                terms = [own1.at[n % SLOTS, b], sums.at[b]]
                if s == 2:
                    terms.append(t1(k, i, DIRS.index(d)).at[b])
                add_into(sums.at[b], span[k][i][1], terms)
            p_copy(k, s, i, d).start()

    def q_target(s, i, d):
        hf = 1 if d == 1 else 0
        p = pos[1 - i]
        return (at(p + 2), hf) if s == 0 else (at(p + d), 1 - hf if s == 1 else hf)

    def q_rows(ref, k, i, p, h):
        lo, n = cuts[k][i][h]
        return (ref.at[pos[0], p] if i == 0 else ref.at[p, pos[1]]).at[pl.ds(lo, n)]

    def q_copy(k, s, i, d):
        di = DIRS.index(d)
        p, h = q_target(s, i, d)
        dst = t2(k, i, d) if s == 0 else r2(k, i, di, h)
        return remote(q_rows(land(k), k, i, p, h), dst, s_rs.at[k], r_q.at[k, s, i, di], device(1 - i, d))

    def q_terms(k, i, p, h):
        off, n = cuts[k][i][h][0] - span[k][i][0], cuts[k][i][h][1]
        rows = pl.ds(off, n)
        return [own2.at[i, p, rows], q_rows(land(k), k, i, p, h)] + [r1(k, i, di, p).at[rows] for di in CORES]

    def stage_q(k, s):
        if s == 0:
            for i in CORES:
                own2_copy(k, i).wait()
                pair_copy(k, 12 + i).wait_recv()
            for i, d in pieces:
                p_copy(k, 1, i, d).wait_recv()
                p_copy(k, 2, i, d).wait_recv()
        for i, d in pieces:
            p, h = q_target(s, i, d)
            terms = q_terms(k, i, p, h)
            if s == 2:
                q_copy(k, 0, i, d).wait_recv()
                terms.append(t2(k, i, d))
            add_into(q_rows(land(k), k, i, p, h), cuts[k][i][h][1], terms)
            q_copy(k, s, i, d).start()

    def moment_refs(k):
        return m_out[max(k, IN_HBM)], v_out[max(k, IN_HBM)]

    def step_loads(k):
        new_m, new_v = moment_refs(k)
        return [local(w[k].at[:, x * side + y], w_raw, s_in.at[0]), local(m[k], new_m, s_in.at[1]), local(v[k], new_v, s_in.at[2])]

    def step_stores(k):
        if k >= IN_HBM:
            return []
        new_m, new_v = moment_refs(k)
        return [local(new_m, m_out[k], s_out.at[0]), local(new_v, v_out[k], s_out.at[1])]

    def own_rows(k, core):
        rows, lanes = forms[k]
        if rows % TILE == 0:
            return core * (rows * lanes), rows * lanes
        return core * (rows // TILE * TILE * lanes), (rows // TILE + 1) * TILE * lanes

    def grad_copy(k):
        lo, n = own_rows(k, other)
        rows = pl.ds(pl.multiple_of(lo, 8), n)
        return remote(grad.at[rows], grad_p.at[rows], s_grad.at[k], r_grad.at[k], partner)

    def x_copies(k):
        rows, lanes = forms[k]
        lo, n = own_rows(k, c)
        if rows % TILE == 0:
            mine = pl.ds(pl.multiple_of(lo, 8), n)
            return [remote(w_all.at[other, mine], w_all.at[other, mine], s_x.at[k, 0], r_x.at[k, 0], partner)]
        tile = TILE * lanes
        mine = pl.ds(pl.multiple_of(c * (n - 2 * tile + 2 * tile), 8), n - tile)
        middle = pl.ds(n - tile, tile)
        return [
            remote(w_all.at[other, mine], w_all.at[other, mine], s_x.at[k, 0], r_x.at[k, 0], partner),
            remote(w_all.at[other, middle], shared, s_x.at[k, 1], r_x.at[k, 1], partner),
        ]

    def take_step(k):
        rows, lanes = forms[k]

        def update(core):
            grads = (grad, grad_p) if core == 0 else (grad_p, grad)
            m_ref, v_ref = moment_refs(k)

            def one(layer, at_w, at_m):
                new_w, new_m, new_v = moments(w_all[layer, at_w, :], m_ref[at_m, :], v_ref[at_m, :], grads[layer][at_w, :])
                w_all[layer, at_w, :] = new_w
                m_ref[at_m, :] = new_m
                v_ref[at_m, :] = new_v

            if rows % TILE == 0:
                size = rows * lanes
                chunk = 8 * (rows // TILE)

                def body(n, _):
                    for layer in CORES:
                        one(layer, pl.ds(pl.multiple_of(core * size + n * chunk, 8), chunk), pl.ds(pl.multiple_of(layer * size + n * chunk, 8), chunk))
                    return 0

                lax.fori_loop(0, lanes, body, 0)
            else:
                first, last = core * rows, (core + 1) * rows
                parts = []
                r = first
                while r < last:
                    n = min(8 - r % 8, last - r)
                    parts.append((r, n))
                    r += n

                def body(lane, _):
                    for layer in CORES:
                        for r, n in parts:
                            one(layer, pl.ds((r // TILE * lanes + lane) * 8 + r % 8, n), pl.ds((r - first) * 2 * lanes + lane * 2 + layer, n, stride=2 * lanes))
                    return 0

                lax.fori_loop(0, lanes, body, 0)

        for core in CORES:
            pl.when(c == core)(functools.partial(update, core))

    def stage_step(k):
        loads = step_loads(k)
        loads[0].wait()
        for layer in CORES:

            def widen(start, size, layer=layer):
                w_all[layer, pl.ds(start, size), :] = w_raw[layer, pl.ds(start, size), :].astype(F32)

            loop(block, widen)
        for i, d in pieces:
            q_copy(k, 1, i, d).wait_recv()
            q_copy(k, 2, i, d).wait_recv()
        for i in CORES:
            for h in CORES:
                lo, n = cuts[k][i][h]
                terms = q_terms(k, i, pos[1 - i], h) + [r2(k, i, di, h) for di in CORES]
                add_into(grad.at[pl.ds(lo, n)], n, terms, F32)
        grad_copy(k).start()
        local(most(k), most(k), s_rs.at[k]).wait()
        for to in neighbours:
            pl.semaphore_signal(free.at[k], inc=1, device_id=to, device_id_type=MESH)
        loads[1].wait()
        loads[2].wait()
        grad_copy(k).wait_recv()
        take_step(k)
        for copy in step_stores(k):
            copy.start()
        swaps = x_copies(k)
        for copy in swaps:
            copy.start()
        for copy in swaps:
            copy.wait()
        rows, lanes = forms[k]
        if rows % TILE:
            tile = TILE * lanes
            start = rows // TILE * tile

            def merge(n, _):
                here = pl.ds(pl.multiple_of(start + n * 8, 8), 8)
                theirs = shared[pl.ds(pl.multiple_of(n * 8, 8), 8), :]
                mine = w_all[c, here, :]
                low = lax.broadcasted_iota(jnp.int32, theirs.shape, 0) < rows % TILE
                w_all[c, here, :] = jnp.where(low == (c == 0), mine, theirs)
                return 0

            lax.fori_loop(0, lanes, merge, 0)

        def narrow(start, size):
            out[k][c, x, y, pl.ds(start, size), :] = w_all[c, pl.ds(start, size), :].astype(BF16)

        loop(block, narrow)
        grad_copy(k).wait_send()
        for copy in step_stores(k):
            copy.wait()

    def place(i, first, second):
        return (second, first) if i == 0 else (first, second)

    def rows_of(k, i, h):
        return pl.ds(*(span[k][i] if h is None else cuts[k][i][h]))

    def ag_copy(k, i, along, d, first, second, h, event):
        dst = out[k].at[c, *place(i, first, second), rows_of(k, i, h)]
        return remote(dst, dst, s_ag.at[k], r_ag.at[k, i, event], device(1 - i if along == 0 else i, d))

    def fan(k, i, first, second, h):
        there = out[k].at[c, *place(i, first, second), rows_of(k, i, h)]
        remote(there, there, s_fan.at[k], r_fan.at[k], partner).start()

    def arrived(k, i, first, second, h, event):
        ag_copy(k, i, 0, 1, first, second, h, event).wait_recv()

    def ag_own(k):
        src = out[k].at[c, x, y]
        pl.semaphore_wait(free.at[k], len(neighbours))
        for i in CORES:
            f, s = pos[1 - i], pos[i]
            for di, d in enumerate(DIRS):
                ag_copy(k, i, 0, d, f, s, None, di).start()
            for di, d in enumerate(DIRS):
                ag_copy(k, i, 1, d, f, s, None, 4 + 5 * di).start()
        remote(src, src, s_fan.at[k], r_fan.at[k], partner).start()

    def ag_near(k):
        for di, d in enumerate(DIRS):
            for i in CORES:
                f, s = pos[1 - i], pos[i]
                from_ = at(f - d)
                arrived(k, i, from_, s, None, di)
                ag_copy(k, i, 0, d, from_, s, 1 - di, 2 + di).start()
                for d2i, d2 in enumerate(DIRS):
                    ag_copy(k, i, 1, d2, from_, s, None, 4 + 5 * d2i + 1 + di).start()
                fan(k, i, from_, s, None)

    def ag_far(k):
        for di, d in enumerate(DIRS):
            for i in CORES:
                f, s = pos[1 - i], pos[i]
                arrived(k, i, at(f + 2), s, 1 - di, 2 + di)
                for d2i, d2 in enumerate(DIRS):
                    ag_copy(k, i, 1, d2, at(f + 2), s, 1 - di, 4 + 5 * d2i + 3 + 1 - di).start()
                fan(k, i, at(f + 2), s, 1 - di)

    kinds = ((0, None, 0, 14), (-1, None, 0, 15), (1, None, 1, 16), (2, 0, 1, 17), (2, 1, 1, 18))

    def ag_second(k, n):
        rel, h, onward, event = kinds[n]
        for di, d in enumerate(DIRS):
            for i in CORES:
                f, s = pos[1 - i], pos[i]
                first, second = at(f + rel), at(s - d)
                arrived(k, i, first, second, h, 4 + 5 * di + n)
                if di == onward:
                    ag_copy(k, i, 1, d, first, second, h, event).start()
                fan(k, i, first, second, h)

    def ag_last(k, n):
        rel, h, _, event = kinds[n]
        for i in CORES:
            f, s = pos[1 - i], pos[i]
            arrived(k, i, at(f + rel), at(s + 2), h, event)
            fan(k, i, at(f + rel), at(s + 2), h)

    neighbours = [device(i, d) for i in CORES for d in DIRS]
    barrier = pltpu.get_barrier_semaphore()
    for to in (partner, *neighbours):
        pl.semaphore_signal(barrier, inc=1, device_id=to, device_id_type=MESH)
    for n in range(SLOTS):
        own1_copy(n).start()
    for i in CORES:
        own2_copy(0, i).start()
    pl.semaphore_wait(barrier, 1 + len(neighbours))
    for b, h in quarters:
        for i, d in pieces:
            first_pair(i, d, b, h).start()
    for k in WEIGHTS:
        for j in range(0 if k else len(pieces), 14):
            pair_copy(k, j).start()

    def stage_q_with_loads(k, s):
        if s == 0:
            for copy in step_loads(k):
                copy.start()
        stage_q(k, s)

    def stage_f(k):
        stage_step(k)
        if k + 1 < len(WEIGHTS):
            for i in CORES:
                own2_copy(k + 1, i).start()

    tasks = {"P": stage_p, "Q": stage_q_with_loads, "F": stage_f, "O": ag_own, "N": ag_near, "X": ag_far, "S": ag_second, "L": ag_last}
    for line in SCHEDULE:
        for task in line.split():
            tasks[task[0]](*(int(digit) for digit in task[1:]))

    for k in WEIGHTS:
        whole = land(k)
        local(whole, whole, s_pair.at[k]).wait()
        local(most(k), most(k), s_ag.at[k]).wait()
        local(whole, whole, s_fan.at[k]).wait()
        local(whole, whole, r_fan.at[k]).wait()


def deliver(*refs):
    n = (len(refs) - 4) // 2
    src, dst, (buffer, s_in, s_out, s_pass) = refs[:n], refs[n : 2 * n], refs[2 * n :]
    through = [j for j in range(len(WEIGHTS), n) if j % len(WEIGHTS) < IN_HBM]
    copies = []
    for at, j in enumerate(through):
        pltpu.make_async_copy(src[j], buffer.at[at], s_in.at[at]).start()
    for j in range(n):
        if j in through:
            continue
        if j < len(WEIGHTS):
            for core in CORES:
                for x in range(src[j].shape[1]):
                    pltpu.make_async_copy(src[j].at[core, x], dst[j].at[core, x], s_out.at[j]).start()
        else:
            pltpu.make_async_copy(src[j], dst[j], s_out.at[j]).start()
        copies.append(pltpu.make_async_copy(src[j], dst[j], s_out.at[j]))
    for at, j in enumerate(through):
        pltpu.make_async_copy(src[j], buffer.at[at], s_in.at[at]).wait()
        copies.append(pltpu.make_async_copy(buffer.at[at], dst[j], s_pass.at[at]))
        copies[-1].start()
    for copy in copies:
        copy.wait()


def tiles(a, chips):
    layers, rows, columns = a.shape
    a = a.reshape(layers, rows // TILE, TILE, columns // LANES, LANES).transpose(0, 1, 3, 2, 4)
    return a.reshape(layers, chips, -1, LANES)


def untiles(a, shape):
    layers, rows, columns = shape
    a = a.reshape(layers, rows // TILE, columns // LANES, TILE, LANES).transpose(0, 1, 3, 2, 4)
    return a.reshape(shape)


def moment_rows(a):
    layers, rows, columns = a.shape
    if rows % TILE == 0:
        return tiles(a, 1).reshape(-1, LANES)
    a = with_layout_constraint(a.reshape(layers, rows, columns // LANES, LANES), Layout(major_to_minor=(1, 2, 0, 3)))
    return a.transpose(1, 2, 0, 3).reshape(-1, LANES)


def moment_back(a, shape):
    layers, rows, columns = shape
    if rows % TILE == 0:
        return untiles(a, shape)
    return a.reshape(rows, columns // LANES, layers, 128).transpose(0, 2, 1, 3).reshape(rows, layers, columns).transpose(1, 0, 2)


def solution(mesh):
    n = mesh.shape["dp"]
    side = math.isqrt(n // 2)
    chips = side * side
    assert 2 * chips == n and side == 4

    def step(*arrays):
        terms, weights, m, v = (arrays[i : i + 3] for i in (0, 3, 6, 9))
        shapes, m_shapes = [a.shape for a in weights], [a.shape for a in m]
        block = math.prod(shapes[0][1:]) // chips // LANES
        forms = [(s[1], s[2] // LANES) for s in m_shapes]
        wide = max(sum(h[1] for h in i) for i in ranges(block, 0))
        odd = max([lanes * TILE for rows, lanes in forms if rows % TILE] + [8])
        split = (2, side, side, block, LANES)
        operands = (
            [tiles(t[0], chips).reshape(split) for t in terms] + [tiles(a, chips) for a in weights] + [moment_rows(a) for a in m + v]
        )
        dma = pltpu.SemaphoreType.DMA
        moment = jax.ShapeDtypeStruct(operands[6].shape, F32)
        anywhere, vmem = pl.BlockSpec(memory_space=pl.ANY), pl.BlockSpec(memory_space=pltpu.VMEM)
        made = pl.pallas_call(
            functools.partial(kernel, side, block, forms),
            out_shape=[pltpu.VMEM(split, BF16)] * 3 + ([moment] * IN_HBM + [pltpu.VMEM(moment.shape, F32)] * (3 - IN_HBM)) * 2,
            in_specs=[anywhere] * 12,
            out_specs=[vmem] * 3 + ([anywhere] * IN_HBM + [vmem] * (3 - IN_HBM)) * 2,
            scratch_shapes=[
                pltpu.VMEM((SLOTS, 2, wide, LANES), BF16),
                pltpu.VMEM((2, side, wide, LANES), BF16),
                pltpu.VMEM((block, LANES), F32),
                pltpu.VMEM((block, LANES), F32),
                pltpu.VMEM((2, block, LANES), BF16),
                pltpu.VMEM((2, block, LANES), F32),
                pltpu.VMEM((odd, LANES), F32),
                *(dma(shape) for shape in ((3,), (3, 14), (SLOTS,), (2,), (3,), (3, 3, 2, 2), (3, 3, 2, 2), (3,), (3,), (3,), (3, 2), (3, 2), (2,), (3,), (3, 2, 19), (3,), (3,), (2,) * 5)),
                pltpu.SemaphoreType.REGULAR((3,)),
            ],
            compiler_params=pltpu.CompilerParams(collective_id=0, has_side_effects=True, vmem_limit_bytes=VMEM_MAIN),
        )(*operands)
        made = [a if j >= 3 and j % 3 < IN_HBM else pltpu.with_memory_space_constraint(a, pltpu.VMEM) for j, a in enumerate(made)]
        results = pl.pallas_call(
            deliver,
            out_shape=[jax.ShapeDtypeStruct(a.shape, a.dtype) for a in made],
            in_specs=[anywhere] * 9,
            out_specs=[anywhere] * 9,
            scratch_shapes=[pltpu.VMEM((2 * IN_HBM, *moment.shape), F32), dma((2 * IN_HBM,)), dma((len(made),)), dma((2 * IN_HBM,))],
            compiler_params=pltpu.CompilerParams(vmem_limit_bytes=VMEM_MAIN),
        )(*made)
        new = [untiles(a, s) for a, s in zip(results[:3], shapes, strict=True)]
        return (*new, *(moment_back(a, s) for a, s in zip(results[3:], m_shapes * 2, strict=True)))

    all_of, cut = P(None, None, None), P(None, "dp", None)
    return jax.shard_map(
        step,
        mesh=mesh,
        in_specs=(P(("rep", "dp"), None, None, None),) * 3 + (all_of,) * 3 + (cut,) * 6,
        out_specs=(P("rep", None, None),) * 3 + (P("rep", "dp", None),) * 6,
        check_vma=False,
    )
```

time: 308 us -> 301 us (0.977)
  Pallas kernels: 307 us -> 300 us
    pallas_call x1 -> x0, Pallas kernels: 4.57 us -> none  [moment_rows(): pl.pallas_call(spread, out_shape=[jax.ShapeDtypeStruct(shape, F32) for sh...]
where the time goes in v2:
time: 301 us; the launch traced here: 300 us
  Pallas kernels  300 us (100%)
    pallas_call x1, Pallas kernels, step(): pl.pallas_call(functools.partial(kernel, side, block, forms), out_shape=[...  281 us
    pallas_call x1, Pallas kernels, step(): pl.pallas_call(deliver, out_shape=[jax.ShapeDtypeStruct(a.shape, a.dtype)...  18.8 us

profile of v2, /device:TPU:97, one launch (start us, length us, event | category | flops | bytes accessed | tf_op | source)
XLA Modules:
  0.0 300.5 jit_solution(16102387533978344195)
XLA Ops:
  0.6 281.0 %shard_map.187 = (bf16[2,4,4,2128,128]{4,3,2,1,0:T(8,128)(2,1)S(1)}, bf16[2,4,4,2128,128]{4,3,2,1,0:T(8,128)(2,1)S(1)}, bf16[2,4,4,2128,128]{4,3,2,1,0:T(8,128)(...) custom-call(bf16[2,4,4,2128,128]{4,3,2,1,0:T(8,128)(2,1)} %bitcast.1, ...), custom_call_target="tpu_custom_call" | custom-call | tf_op jit(solution)/shard_map/pallas_call | solution.py:567
  281.7 18.8 %shard_map.188 = (bf16[2,4,4,2128,128]{4,3,2,1,0:T(8,128)(2,1)}, bf16[2,4,4,2128,128]{4,3,2,1,0:T(8,128)(2,1)}, bf16[2,4,4,2128,128]{4,3,2,1,0:T(8,128)(2,1)}, f...) custom-call(bf16[2,4,4,2128,128]{4,3,2,1,0:T(8,128)(2,1)S(1)} %get-t, ...), custom_call_target="tpu_custom_call" | custom-call | tf_op jit(solution)/shard_map/pallas_call | solution.py:586

commit v3 on v2

--- a/solution.py
+++ b/solution.py
@@ -21,18 +21,18 @@
     "P00 P01 P02 P10",
     "P11 Q00 Q01 P12",
     "Q02 P20 P21 F0",
-    "Q10 Q11 O0 P22",
-    "Q12 N0 F1 Q20",
-    "S02 X0 Q21 Q22",
-    "O1 N1 S01 F2",
-    "S00 O2 S03 S04",
-    "L02 X1 L01 S10",
-    "N2 L04 L00 S14",
-    "L03 S11 S12 S13",
-    "X2 S20 L10 L14",
-    "L13 L12 L11 S21",
-    "S22 S23 S24 L21",
-    "L20 L22 L23 L24",
+    "O0 Q10 Q11 P22",
+    "Q12 N0 F1 O1",
+    "Q20 Q21 X0 Q22",
+    "S00 S01 S02 S03",
+    "S04 F2 O2 N1",
+    "X1 N2 L00 L02",
+    "L01 L03 L04 S10",
+    "S11 S12 S13 S14",
+    "X2 L10 L12 L11",
+    "L13 L14 S20 S21",
+    "S22 S23 S24 L20",
+    "L22 L21 L23 L24",
 )
 
 

time: 301 us -> 299 us (level)
  no operation moved by 1% of the time
where the time goes in v3:
time: 299 us
  Pallas kernels  298 us (100%)
    pallas_call x1, Pallas kernels, step(): pl.pallas_call(functools.partial(kernel, side, block, forms), out_shape=[...  279 us
    pallas_call x1, Pallas kernels, step(): pl.pallas_call(deliver, out_shape=[jax.ShapeDtypeStruct(a.shape, a.dtype)...  18.8 us

profile of v3, /device:TPU:97, one launch (start us, length us, event | category | flops | bytes accessed | tf_op | source)
XLA Modules:
  0.0 298.9 jit_solution(5119987866456159379)
XLA Ops:
  0.6 279.5 %shard_map.187 = (bf16[2,4,4,2128,128]{4,3,2,1,0:T(8,128)(2,1)S(1)}, bf16[2,4,4,2128,128]{4,3,2,1,0:T(8,128)(2,1)S(1)}, bf16[2,4,4,2128,128]{4,3,2,1,0:T(8,128)(...) custom-call(bf16[2,4,4,2128,128]{4,3,2,1,0:T(8,128)(2,1)} %bitcast.1, ...), custom_call_target="tpu_custom_call" | custom-call | tf_op jit(solution)/shard_map/pallas_call | solution.py:567
  280.1 18.8 %shard_map.188 = (bf16[2,4,4,2128,128]{4,3,2,1,0:T(8,128)(2,1)}, bf16[2,4,4,2128,128]{4,3,2,1,0:T(8,128)(2,1)}, bf16[2,4,4,2128,128]{4,3,2,1,0:T(8,128)(2,1)}, f...) custom-call(bf16[2,4,4,2128,128]{4,3,2,1,0:T(8,128)(2,1)S(1)} %get-t, ...), custom_call_target="tpu_custom_call" | custom-call | tf_op jit(solution)/shard_map/pallas_call | solution.py:586
